TPU v7x, 32 devices: a whole 2x2x4 slice. The times are simulated.
32 devices in a mesh: rep: 2 (over y), seq: 4 (over z), tp: 4 (over x, core).
Axes of the slice: x: 2, y: 2, z: 4, core: 2. Of those that a mesh axis runs over, the one named last changes fastest.
Arguments:
- queries: bfloat16 [128, 64, 128], P(('rep', 'seq')), parts along dimension 0, may hold values from -9 to 9
- key_pages: bfloat16 [1024, 8, 64, 128], P(('rep', 'seq'), 'tp'), parts along dimension 0, may hold values from -4 to 4
- value_pages: bfloat16 [1024, 8, 64, 128], P(('rep', 'seq'), 'tp'), parts along dimension 0, may hold values from -6 to 6
- page_owner: int32 [128, 128], P('rep'), parts along dimension 0, may hold values from 0 to 3, as said below
- page_local: int32 [128, 128], P('rep'), parts along dimension 0, may hold values from 0 to 127, as said below
- seq_lengths: int32 [128], P('rep'), parts along dimension 0, may hold values from 1 to 8192, as said below
Outputs:
- attention: bfloat16 [128, 64, 128], P(('rep', 'seq'), 'tp'), parts along dimension 0
There are 2 independent parts, one for each index of `rep`. A program takes and returns all parts, laid end to end along the dimension named above; each array names one. Nothing has to cross between parts.
Inputs may be any that keep to these rules, and one draw needn't show every extreme that they name: The live slots (s * 64 < seq_lengths[b]) name pairs (page_owner, page_local) that are all different; the other slots hold 0. `page_local`: see page_owner. `seq_lengths`: one sequence has exactly 8192 tokens; the live slots of all sequences together number at most half of the 512 pages.
All inputs are finite; a program needn't handle non-finite values.
Results may differ from a plain program's by a relative error of at most 0.008.
Values may be sent and summed in bfloat16 or wider, within the bound.
A program may use at most 64 MiB of HBM per device.

v0:
```python
import math

import jax
import jax.numpy as jnp
from jax import lax
from jax.sharding import PartitionSpec as P

HQ = 64
KVH = 8


score_shift = 8.0


def body(queries, key_pages, value_pages, page_owner, page_local, seq_lengths):
    seq_count = page_owner.shape[0]
    slot_count = page_owner.shape[1]
    pool_pages = key_pages.shape[0]
    kv_local = key_pages.shape[1]
    page_len = key_pages.shape[2]
    head_dim = key_pages.shape[3]
    group_size = HQ // KVH
    heads_local = kv_local * group_size
    seq_rank = lax.axis_index("seq")
    tp_rank = lax.axis_index("tp")
    slot_ids = jnp.arange(slot_count, dtype=jnp.int32)
    slot_fill = jnp.clip(seq_lengths[:, None] - slot_ids[None, :] * page_len, 0, page_len)
    owned = (slot_fill > 0) & (page_owner == seq_rank)
    pool_range = jnp.arange(pool_pages, dtype=jnp.int32)
    matches = ((page_local[:, :, None] == pool_range[None, None, :]) & owned[:, :, None]).astype(
        jnp.bfloat16
    )
    fill_weight = slot_fill.astype(jnp.bfloat16)
    fill_table = jnp.einsum("bsp,bs->bp", matches, fill_weight, preferred_element_type=jnp.float32)
    hit_table = jnp.sum(matches.astype(jnp.float32), axis=1)
    seq_weight = jnp.arange(seq_count, dtype=jnp.float32)
    page_seq = jnp.dot(seq_weight, hit_table, precision=lax.Precision.HIGHEST).astype(jnp.int32)
    page_fill = jnp.sum(fill_table, axis=0).astype(jnp.int32)
    local_heads = lax.dynamic_slice_in_dim(queries, tp_rank * heads_local, heads_local, 1)
    head_queries = lax.all_gather(local_heads, "seq", axis=0, tiled=True)
    query_flat = head_queries.reshape(seq_count, heads_local * head_dim)
    score_scale = 1.0 / math.sqrt(head_dim)
    seq_range = jnp.arange(seq_count, dtype=jnp.int32)
    count = page_seq.shape[0]
    selector = page_seq[:, None] == seq_range[None, :]
    picked = jnp.dot(
        selector.astype(jnp.bfloat16), query_flat, preferred_element_type=jnp.float32
    ).astype(jnp.bfloat16)
    picked = picked.reshape(count, kv_local, group_size, head_dim)
    scores = (
        jnp.einsum("pkgd,pktd->pkgt", picked, key_pages, preferred_element_type=jnp.float32)
        * score_scale
    )
    live_mask = jnp.arange(page_len, dtype=jnp.int32)[None, :] < page_fill[:, None]
    weight = jnp.where(live_mask[:, None, None, :], jnp.exp(scores - score_shift), 0.0)
    page_total = jnp.sum(weight, axis=-1)
    page_sum = jnp.einsum(
        "pkgt,pktd->pkgd",
        weight.astype(jnp.bfloat16),
        value_pages,
        preferred_element_type=jnp.float32,
    )
    spread = selector.astype(jnp.float32).T
    numerator = jnp.dot(
        spread, page_sum.reshape(count, heads_local * head_dim), precision=lax.Precision.HIGHEST
    )
    denominator = jnp.dot(
        spread, page_total.reshape(count, heads_local), precision=lax.Precision.HIGHEST
    )
    numerator, denominator = (numerator, denominator)
    own_rows = seq_count // lax.axis_size("seq")
    summed_num, summed_den = lax.psum((numerator, denominator), "seq")
    summed_num = lax.dynamic_slice_in_dim(summed_num, seq_rank * own_rows, own_rows, 0)
    summed_den = lax.dynamic_slice_in_dim(summed_den, seq_rank * own_rows, own_rows, 0)
    result = summed_num.reshape(own_rows, heads_local, head_dim) / summed_den[..., None]
    return result.astype(jnp.bfloat16)


def solution(mesh):
    placed = (
        P(("rep", "seq"), None, None),
        P(("rep", "seq"), "tp", None, None),
        P(("rep", "seq"), "tp", None, None),
        P("rep", None),
        P("rep", None),
        P("rep"),
    )
    return jax.shard_map(
        body, mesh=mesh, in_specs=placed, out_specs=P(("rep", "seq"), "tp", None), check_vma=False
    )
```

profile of v0, /device:TPU:0, one launch (start us, length us, event | category | flops | bytes accessed | tf_op | source)
XLA Modules:
  0.0 89.1 jit_solution(877653192962036179)
XLA Ops:
  6.5 0.0 copy-start
  6.5 0.0 all-reduce.2.cloned.1.call-start
  6.5 0.8 fusion.35
  7.3 0.8 fusion.34
  8.2 4.5 %convert_reduce_fusion = f32[64,128]{1,0:T(8,128)S(1)} fusion(s32[64,128]{1,0:T(8,128)} %param.10, pred[64,128]{1,0:T(8,128)(4,1)S(1)} %fusion.34), kind=kLoop, calls=%fused_computation | loop fusion | flops 5234688 | bytes 73728 | tf_op jit(solution)/shard_map/reduce_sum | solution.py:35
  12.7 3.1 %fusion.14 = s32[128]{0:T(128)S(1)} fusion(s32[64,128]{1,0:T(8,128)} %param.10, pred[64,128]{1,0:T(8,128)(4,1)S(1)} %fusion.34, bf16[64,128,1]{1,0,2:T(8,128)(2,1)S(1)} %fusion.35), kind=kOutput, calls=%fused_computation.16 | convolution fusion | flops 4194432 | bytes 57856 | tf_op jit(solution)/shard_map/bsp,bs->bp/dot_general | solution.py:34
  15.8 0.1 iota_compare_fusion.1
  15.9 0.1 fusion.10
  16.0 0.0 copy-done
  16.0 0.0 copy-start.1
  16.1 15.8 %all_gather.3 = bf16[64,16,128]{2,1,0:T(8,128)(2,1)S(1)} all-gather(bf16[16,16,128]{2,1,0:T(8,128)(2,1)S(1)} %constant_dynamic-slice_fusion.1), channel_id=1, replica_groups=mesh['rep'=2,'seq'=4,'tp'=4] {'seq'}, dimensions={0}, use_global_device_ids=true | all-gather | bytes 327680 | tf_op jit(solution)/shard_map/all_gather | solution.py:40
  31.9 0.3 fusion.9
  32.2 0.1 copy.11
  32.3 4.6 %fusion.38 = (f32[128,2,8]{2,1,0:T(2,128)S(1)}, bf16[128,2,8,64]{3,2,1,0:T(8,128)(2,1)S(1)}) fusion(bf16[128,2,8,128]{3,2,1,0:T(8,128)(2,1)S(1)} %bitcast.38, bf16[128,2,64,128]{3,2,1,0:T(8,128)(2,1)} %param.7, pred[128,64]{1,0:T(8,128)(4,1)S(1)} %iota_compare_fusion.1), kind=kOutput, calls=%fused_computation.45 | convolution fusion | flops 34207744 | bytes 4997120 | tf_op jit(solution)/shard_map/pkgd,pktd->pkgt/dot_general | solution.py:51
  37.0 0.0 copy-done.1
  37.0 1.2 %fusion.20 = f32[128,2,8,128]{3,2,1,0:T(8,128)S(1)} fusion(bf16[128,2,64,128]{3,2,1,0:T(8,128)(2,1)S(1)} %copy-done.1, bf16[128,2,8,64]{3,2,1,0:T(8,128)(2,1)S(1)} %get-tuple-element.6), kind=kOutput, calls=%fused_computation.20 | convolution fusion | flops 33554432 | bytes 5505024 | tf_op jit(solution)/shard_map/pkgt,pktd->pkgd/dot_general | solution.py:57
  38.2 1.7 %fusion.17 = f32[64,2048]{1,0:T(8,128)} fusion(f32[16,8,16,128]{3,2,1,0:T(8,128)S(1)} %bitcast.37, s32[128]{0:T(128)S(1)} %fusion.10), kind=kOutput, calls=%fused_computation.17 | convolution fusion | flops 201334784 | bytes 1573376 | tf_op jit(solution)/shard_map/dot_general | solution.py:64
  39.8 0.0 all-reduce.2.cloned.1.call-update
  39.8 0.1 copy.8
  39.9 0.3 fusion.26
  40.2 20.0 %psum.15 = f32[64,16]{1,0:T(8,128)S(1)} all-reduce(f32[64,16]{1,0:T(8,128)S(1)} %fusion.26), channel_id=1, replica_groups=mesh['rep'=2,'seq'=4,'tp'=4] {'seq'}, use_global_device_ids=true, to_apply=%region_3.4 | all-reduce | flops 1024 | bytes 8192 | tf_op jit(solution)/shard_map/psum | solution.py:72
  60.2 20.3 %all-reduce.2.cloned.1.call-done = f32[64,2048]{1,0:T(8,128)} async-done(((f32[64,2048]{1,0:T(8,128)}), f32[64,2048]{1,0:T(8,128)}) %all-reduce.2.cloned.1.call-update) | async-done | bytes 524304 | tf_op jit(solution)/shard_map/psum | solution.py:72
  80.6 0.9 %dynamic-slice_bitcast_fusion = f32[2,8,16,128]{3,1,2,0:T(8,128)S(1)} fusion(f32[64,2048]{1,0:T(8,128)} %all-reduce.2.cloned.1.call-done, s32[]{:T(128)S(6)} %select_n.13), kind=kLoop, calls=%fused_computation.26 | loop fusion | bytes 262148
  81.5 0.7 fusion.24
  (4 shorter events, 0.1 us)
Async XLA Ops:
  6.5 9.5 %copy-start = (bf16[16,64,128]{2,1,0:T(8,128)(2,1)S(1)}, bf16[16,64,128]{2,1,0:T(8,128)(2,1)}, u32[]{:S(2)}) copy-start(bf16[16,64,128]{2,1,0:T(8,128)(2,1)} %param.6) | copy-start | bytes 786436
  6.5 74.0 %all-reduce.2.cloned.1.call-start = ((), (), s32[]{:S(2)}) async-start(), calls=%async_computation | async-start | bytes 1048576 | tf_op jit(solution)/shard_map/psum | solution.py:72
  16.0 20.9 %copy-start.1 = (bf16[128,2,64,128]{3,2,1,0:T(8,128)(2,1)S(1)}, bf16[128,2,64,128]{3,2,1,0:T(8,128)(2,1)}, u32[]{:S(2)}) copy-start(bf16[128,2,64,128]{3,2,1,0:T(8,128)(2,1)} %param.8) | copy-start | bytes 12582916
Sparse Core Ops, SparseCore 0:
  40.0 40.5 all-reduce.1
where the time goes:
time: 89.6 us; the launch traced here: 89.1 us
  blocking collectives  35.8 us (40%)
  waiting for transfers between devices  20.3 us (23%)
  between operations  13.5 us (15%)
  matrix products  11.4 us (13%)
  other arithmetic  6.96 us (8%)
  local copies, waits for them, and re-layouts  1.15 us (1%)
    psum x1, waiting for transfers between devices, body(): summed_num, summed_den = lax.psum((numerator, denominator), 'seq')  20.3 us
    psum x1, blocking collectives, body(): summed_num, summed_den = lax.psum((numerator, denominator), 'seq')  20 us
    all_gather x1, blocking collectives, body(): head_queries = lax.all_gather(local_heads, 'seq', axis=0, tiled=True)  15.8 us
    dot_general x1, matrix products, body(): jnp.einsum('pkgd,pktd->pkgt', picked, key_pages, preferred_element_type=j...  4.63 us
    reduce_sum x1, other arithmetic, body(): hit_table = jnp.sum(matches.astype(jnp.float32), axis=1)  4.51 us
    dot_general x1, matrix products, body(): jnp.einsum('bsp,bs->bp', matches, fill_weight, preferred_element_type=jnp...  3.1 us
  transfers between devices with their start and end apart: 1, of which 1 were waited for; matrix products, arithmetic and copies ran while one was open for 0% of the time, Pallas kernels for 0%

commit v1 on v0

v1 whole, which is shorter than its diff:
```python
import functools
import math

import jax
import jax.numpy as jnp
from jax import lax
from jax.experimental import pallas as pl
from jax.experimental.pallas import tpu as pltpu
from jax.sharding import PartitionSpec as P

HQ = 64
KVH = 8
LANES = 128
BLOCK = 8
MESH = pl.DeviceIdType.MESH

score_shift = 8.0


def kernel(
    n, q_hbm, k_hbm, v_hbm, owner_hbm, local_hbm, lens, out_ref,
    kbuf, vbuf, owner, local, qg, qf, qp, fills, onehot, spread, pages, tots, stage, sbuf, rbuf, outf,
    load_sem, qload_sem, kv_sem, qsend_sem, qrecv_sem, osend_sem, orecv_sem,
):
    me = lax.axis_index("seq")
    tp = lax.axis_index("tp")
    pool, kv_local, page_len, dim = k_hbm.shape
    seqs, slots = owner_hbm.shape
    group = HQ // KVH
    rows = seqs // n
    bits = page_len.bit_length()
    scale = 1.0 / math.sqrt(dim)

    table_loads = []
    for at in range(0, slots, LANES):
        part = at // LANES
        for i, (src, dst) in enumerate(((owner_hbm, owner), (local_hbm, local))):
            c = pltpu.make_async_copy(src.at[:, pl.ds(at, LANES)], dst.at[part], load_sem.at[i, part])
            c.start()
            table_loads.append(c)
    q_loads = []
    for kv in range(kv_local):
        first = pl.multiple_of((tp * kv_local + kv) * group, group)
        c = pltpu.make_async_copy(q_hbm.at[:, pl.ds(first, group), :], qg.at[kv, me], qload_sem.at[kv])
        c.start()
        q_loads.append(c)
    kv_loads = []
    for kv in range(kv_local):
        ck = pltpu.make_async_copy(k_hbm.at[:, kv], kbuf.at[kv], kv_sem.at[0, kv])
        cv = pltpu.make_async_copy(v_hbm.at[:, kv], vbuf.at[kv], kv_sem.at[1, kv])
        ck.start()
        cv.start()
        kv_loads.append((ck, cv))

    barrier = pltpu.get_barrier_semaphore()
    for off in range(1, n):
        pl.semaphore_signal(barrier, inc=1, device_id={"seq": lax.rem(me + off, n)}, device_id_type=MESH)
    for c in q_loads:
        c.wait()
    pl.semaphore_wait(barrier, n - 1)

    q_sends = []
    for kv in range(kv_local):
        for off in range(1, n):
            c = pltpu.make_async_remote_copy(
                src_ref=qg.at[kv, me],
                dst_ref=qg.at[kv, me],
                send_sem=qsend_sem.at[kv, off],
                recv_sem=qrecv_sem.at[kv, off],
                device_id={"seq": lax.rem(me + off, n)},
                device_id_type=MESH,
            )
            c.start()
            q_sends.append(c)

    for c in table_loads:
        c.wait()
    page_ids = lax.broadcasted_iota(jnp.int32, (pool, LANES), 0)
    lane = lax.broadcasted_iota(jnp.int32, (1, LANES), 1)

    def match(b, acc):
        length = lens[b]
        for at in range(0, slots, LANES):
            own = owner[at // LANES, pl.ds(b, 1), :]
            loc = local[at // LANES, pl.ds(b, 1), :]
            fill = jnp.clip(length - (lane + at) * page_len, 0, page_len)
            code = jnp.where((own == me) & (fill > 0), loc, -1)
            acc = jnp.where(page_ids == code, (b << bits) + fill, acc)
        return acc

    acc = lax.fori_loop(0, seqs, match, jnp.zeros((pool, LANES), jnp.int32), unroll=8)
    code = jnp.max(acc.astype(jnp.float32), axis=1, keepdims=True)
    wide = jnp.broadcast_to(code, (pool, pool))
    tall = jnp.transpose(wide)[:seqs].astype(jnp.int32)
    wide = wide.astype(jnp.int32)
    full = jnp.broadcast_to(wide[:, :1], (pool, LANES)) & ((1 << bits) - 1)
    for g in range(group):
        fills[pl.ds(g, pool, stride=group), :] = full
    seq_wide = wide[:, :seqs]
    onehot[...] = jnp.where(
        (seq_wide > 0) & ((seq_wide >> bits) == lax.broadcasted_iota(jnp.int32, (pool, seqs), 1)), 1.0, 0.0
    ).astype(jnp.bfloat16)
    spread[...] = jnp.where(
        (tall > 0) & ((tall >> bits) == lax.broadcasted_iota(jnp.int32, (seqs, pool), 0)), 1.0, 0.0
    ).astype(jnp.bfloat16)

    pair = 2 * group
    span = 2 * page_len
    row = lax.broadcasted_iota(jnp.int32, (pair, span), 0)
    col = lax.broadcasted_iota(jnp.int32, (pair, span), 1)
    token = jnp.where((row < group) == (col < page_len), jnp.where(col < page_len, col, col - page_len), span)
    row_l = lax.broadcasted_iota(jnp.int32, (pair, LANES), 0)
    col_l = lax.broadcasted_iota(jnp.int32, (pair, LANES), 1)
    head_of = jnp.where(row_l < group, row_l, row_l - group)
    spot = (col_l == head_of) | (col_l == head_of + group)

    def recv(sem, kv, off, ref):
        src = lax.rem(me + n - off, n)
        return pltpu.make_async_remote_copy(
            src_ref=ref.at[kv, src], dst_ref=ref.at[kv, src], send_sem=qsend_sem.at[kv, off],
            recv_sem=sem.at[kv, off], device_id={"seq": src}, device_id_type=MESH,
        )

    o_sends = []
    for kv in range(kv_local):
        for off in range(1, n):
            recv(qrecv_sem, kv, off, qg).wait_recv()
        qf[...] = qg[kv].reshape(seqs * group, dim).astype(jnp.float32)
        for g in range(group):
            mine = qf[pl.ds(g, seqs, stride=group), :].astype(jnp.bfloat16)
            qp[pl.ds(g, pool, stride=group), :] = jnp.dot(
                onehot[...], mine, preferred_element_type=jnp.float32
            )
        for c in kv_loads[kv]:
            c.wait()

        def attend(step, carry):
            for i in range(BLOCK):
                at = step * BLOCK + i
                rows_at = pl.ds(pl.multiple_of(at * pair, pair), pair)
                pages_at = pl.ds(at * 2, 2)
                q = qp[rows_at, :].astype(jnp.bfloat16)
                k = kbuf[kv, pages_at].reshape(span, dim)
                v = vbuf[kv, pages_at].reshape(span, dim)
                s = lax.dot_general(q, k, (((1,), (1,)), ((), ())), preferred_element_type=jnp.float32)
                w = jnp.where(token < fills[rows_at, :], jnp.exp(s * scale - score_shift), 0.0)
                total = jnp.sum(w, axis=1, keepdims=True)
                tots[rows_at, :] = jnp.where(spot, total, 0.0)
                pages[rows_at, :] = jnp.dot(w.astype(jnp.bfloat16), v, preferred_element_type=jnp.float32)
            return carry

        lax.fori_loop(0, pool // (2 * BLOCK), attend, 0)

        def collect(value):
            high = value.astype(jnp.bfloat16)
            low = (value - high.astype(jnp.float32)).astype(jnp.bfloat16)
            return jnp.dot(spread[...], high, preferred_element_type=jnp.float32) + jnp.dot(
                spread[...], low, preferred_element_type=jnp.float32
            )

        page_tot = tots[pl.ds(0, pool, stride=group), :]
        for g in range(1, group):
            page_tot += tots[pl.ds(g, pool, stride=group), :]
        tot = collect(page_tot)
        high = tot.astype(jnp.bfloat16).astype(jnp.float32)
        lanes = lax.broadcasted_iota(jnp.int32, (seqs, LANES), 1)
        tot = jnp.where(lanes < group, high, tot - high)
        for d in range(n):
            stage[kv, d, group * rows : (group + 1) * rows, :] = tot[d * rows : (d + 1) * rows]
        for g in range(group):
            num = collect(pages[pl.ds(g, pool, stride=group), :])
            for d in range(n):
                stage[kv, d, g * rows : (g + 1) * rows, :] = num[d * rows : (d + 1) * rows]
        for d in range(n):
            sbuf[kv, d] = stage[kv, d].astype(jnp.bfloat16)
        for off in range(1, n):
            peer = lax.rem(me + off, n)
            c = pltpu.make_async_remote_copy(
                src_ref=sbuf.at[kv, peer],
                dst_ref=rbuf.at[kv, me],
                send_sem=osend_sem.at[kv, off],
                recv_sem=orecv_sem.at[kv, off],
                device_id={"seq": peer},
                device_id_type=MESH,
            )
            c.start()
            o_sends.append(c)

    for kv in range(kv_local):
        whole = stage[kv, me]
        for off in range(1, n):
            recv(orecv_sem, kv, off, rbuf).wait_recv()
            whole += rbuf[kv, lax.rem(me + n - off, n)].astype(jnp.float32)
        tot = whole[group * rows :]
        for g in range(group):
            den = tot[:, g : g + 1] + tot[:, group + g : group + g + 1]
            outf[pl.ds(kv * group + g, rows, stride=kv_local * group), :] = whole[g * rows : (g + 1) * rows] / den
    out_ref[...] = outf[...].reshape(rows, kv_local * group, dim).astype(jnp.bfloat16)
    for c in q_sends:
        c.wait_send()
    for c in o_sends:
        c.wait_send()


def solution(mesh):
    n = mesh.shape["seq"]

    def body(queries, key_pages, value_pages, page_owner, page_local, seq_lengths):
        pool, kv_local, page_len, dim = key_pages.shape
        seqs, slots = page_owner.shape
        group = HQ // KVH
        rows = seqs // n
        heads = kv_local * group
        part = (group + 1) * rows
        bf16, f32 = jnp.bfloat16, jnp.float32
        anywhere = pl.BlockSpec(memory_space=pl.ANY)
        return pl.pallas_call(
            functools.partial(kernel, n),
            out_shape=jax.ShapeDtypeStruct((rows, heads, dim), bf16),
            in_specs=[anywhere] * 5 + [pl.BlockSpec(memory_space=pltpu.SMEM)],
            out_specs=pl.BlockSpec(memory_space=pltpu.VMEM),
            scratch_shapes=[
                pltpu.VMEM((kv_local, pool, page_len, dim), bf16),
                pltpu.VMEM((kv_local, pool, page_len, dim), bf16),
                pltpu.VMEM((slots // LANES, seqs, LANES), jnp.int32),
                pltpu.VMEM((slots // LANES, seqs, LANES), jnp.int32),
                pltpu.VMEM((kv_local, n, rows, group, dim), bf16),
                pltpu.VMEM((seqs * group, dim), f32),
                pltpu.VMEM((pool * group, dim), f32),
                pltpu.VMEM((pool * group, LANES), jnp.int32),
                pltpu.VMEM((pool, seqs), bf16),
                pltpu.VMEM((seqs, pool), bf16),
                pltpu.VMEM((pool * group, dim), f32),
                pltpu.VMEM((pool * group, LANES), f32),
                pltpu.VMEM((kv_local, n, part, dim), f32),
                pltpu.VMEM((kv_local, n, part, dim), bf16),
                pltpu.VMEM((kv_local, n, part, dim), bf16),
                pltpu.VMEM((rows * heads, dim), f32),
                pltpu.SemaphoreType.DMA((2, slots // LANES)),
                pltpu.SemaphoreType.DMA((kv_local,)),
                pltpu.SemaphoreType.DMA((2, kv_local)),
                pltpu.SemaphoreType.DMA((kv_local, n)),
                pltpu.SemaphoreType.DMA((kv_local, n)),
                pltpu.SemaphoreType.DMA((kv_local, n)),
                pltpu.SemaphoreType.DMA((kv_local, n)),
            ],
            compiler_params=pltpu.CompilerParams(
                collective_id=0, has_side_effects=True, vmem_limit_bytes=48 * 1024 * 1024
            ),
        )(queries, key_pages, value_pages, page_owner, page_local, seq_lengths)

    placed = (
        P(("rep", "seq"), None, None),
        P(("rep", "seq"), "tp", None, None),
        P(("rep", "seq"), "tp", None, None),
        P("rep", None),
        P("rep", None),
        P("rep"),
    )
    return jax.shard_map(
        body, mesh=mesh, in_specs=placed, out_specs=P(("rep", "seq"), "tp", None), check_vma=False
    )
```

time: 89.6 us -> 46.1 us (0.51)
  Pallas kernels: 0 us -> 39.8 us
  blocking collectives: 35.8 us -> 0 us
  waiting for transfers between devices: 20.3 us -> 0 us
  between operations: 13.5 us -> 0.01 us
  matrix products: 11.4 us -> 0 us
  other arithmetic: 6.96 us -> 0 us
  local copies, waits for them, and re-layouts: 1.15 us -> 5.94 us
    pallas_call x0 -> x1, Pallas kernels: none -> 39.8 us  [body(): pl.pallas_call(functools.partial(kernel, n), out_shape=jax.ShapeDtypeStru...]
    psum x1 -> x0, waiting for transfers between devices: 20.3 us -> none  [body(): summed_num, summed_den = lax.psum((numerator, denominator), 'seq')]
    psum x1 -> x0, blocking collectives: 20 us -> none  [body(): summed_num, summed_den = lax.psum((numerator, denominator), 'seq')]
    all_gather x1 -> x0, blocking collectives: 15.8 us -> none  [body(): head_queries = lax.all_gather(local_heads, 'seq', axis=0, tiled=True)]
    dot_general x7 -> x0, matrix products: 11.4 us -> none  [the longest x1 4.63 us: body(): jnp.einsum('pkgd,pktd->pkgt', picked, key_pages, preferred_element_type=j...]
    unnamed x7 -> x11, local copies, waits for them, and re-layouts: 1.06 us -> 5.94 us
    reduce_sum x1 -> x0, other arithmetic: 4.51 us -> none  [body(): hit_table = jnp.sum(matches.astype(jnp.float32), axis=1)]
    convert_element_type x2 -> x0, other arithmetic: 1.51 us -> none  [the longest x1 0.77 us: body(): fill_weight = slot_fill.astype(jnp.bfloat16)]
  transfers between devices with their start and end apart: 1 -> 0, of which waited for: 1 -> 0; matrix products, arithmetic and copies ran while one was open for 0% -> 0% of each run, Pallas kernels for 0% -> 0%
where the time goes in v1:
time: 46.1 us; the launch traced here: 45.8 us
  Pallas kernels  39.8 us (86%)
  local copies, waits for them, and re-layouts  5.94 us (13%)
    pallas_call x1, Pallas kernels, body(): pl.pallas_call(functools.partial(kernel, n), out_shape=jax.ShapeDtypeStru...  39.8 us
    unnamed x11, local copies, waits for them, and re-layouts  5.94 us

profile of v1, /device:TPU:0, one launch (start us, length us, event | category | flops | bytes accessed | tf_op | source)
XLA Modules:
  0.0 45.8 jit_solution(2235324211751759762)
XLA Ops:
  0.0 0.0 copy-start
  0.0 2.2 %copy-done = bf16[128,2,64,128]{3,2,1,0:T(8,128)(2,1)S(1)} copy-done((bf16[128,2,64,128]{3,2,1,0:T(8,128)(2,1)S(1)}, bf16[128,2,64,128]{3,2,1,0:T(8,128)(2,1)}, u32[]{:S(2)}) %copy-start) | copy-done | bytes 4194328
  2.2 0.0 copy-start.1
  2.2 0.9 %copy-done.1 = bf16[16,64,128]{2,1,0:T(8,128)(2,1)S(1)} copy-done((bf16[16,64,128]{2,1,0:T(8,128)(2,1)S(1)}, bf16[16,64,128]{2,1,0:T(8,128)(2,1)}, u32[]{:S(2)}) %copy-start.1) | copy-done | bytes 262168
  3.1 0.0 copy-start.2
  3.1 0.8 %copy-done.2 = s32[64,128]{1,0:T(8,128)S(1)} copy-done((s32[64,128]{1,0:T(8,128)S(1)}, s32[64,128]{1,0:T(8,128)}, u32[]{:S(2)}) %copy-start.2) | copy-done | bytes 32792
  3.9 0.0 copy-start.3
  3.9 0.8 %copy-done.3 = s32[64,128]{1,0:T(8,128)S(1)} copy-done((s32[64,128]{1,0:T(8,128)S(1)}, s32[64,128]{1,0:T(8,128)}, u32[]{:S(2)}) %copy-start.3) | copy-done | bytes 32792
  4.7 0.0 copy-start.4
  4.7 0.7 %copy-done.4 = s32[64]{0:T(128)S(1)} copy-done((s32[64]{0:T(128)S(1)}, s32[64]{0:T(128)}, u32[]{:S(2)}) %copy-start.4) | copy-done | bytes 280
  5.3 39.8 %shard_map.64 = bf16[16,16,128]{2,1,0:T(8,128)(2,1)S(1)} custom-call(bf16[16,64,128]{2,1,0:T(8,128)(2,1)S(1)} %copy-done.1, bf16[128,2,64,128]{3,2,1,0:T(8,128)(2,1)S(1)} %copy-done, bf16[128,2,64,128]{3,2,1,0:T(8,128)(2,1)} %v_hbm.1, s32[64,128]{1,0:T(8,128)S(1)} %copy-done.2, s32[64,128]{1,0:T(8,128)S(1)} %copy-done.3, s32[64]{0:T(128)S(1)} %copy-done.4), custom_call_target="tpu_custom_call" | custom-call | tf_op jit(solution)/shard_map/pallas_call | solution.py:217
  45.1 0.6 %copy.8 = bf16[16,16,128]{2,1,0:T(8,128)(2,1)} copy(bf16[16,16,128]{2,1,0:T(8,128)(2,1)S(1)} %shard_map.64) | data formatting | bytes 131072
Async XLA Ops:
  0.0 2.2 %copy-start = (bf16[128,2,64,128]{3,2,1,0:T(8,128)(2,1)S(1)}, bf16[128,2,64,128]{3,2,1,0:T(8,128)(2,1)}, u32[]{:S(2)}) copy-start(bf16[128,2,64,128]{3,2,1,0:T(8,128)(2,1)} %k_hbm.1) | copy-start | bytes 12582916
  2.2 0.9 %copy-start.1 = (bf16[16,64,128]{2,1,0:T(8,128)(2,1)S(1)}, bf16[16,64,128]{2,1,0:T(8,128)(2,1)}, u32[]{:S(2)}) copy-start(bf16[16,64,128]{2,1,0:T(8,128)(2,1)} %q_hbm.1) | copy-start | bytes 786436
  3.1 0.8 %copy-start.2 = (s32[64,128]{1,0:T(8,128)S(1)}, s32[64,128]{1,0:T(8,128)}, u32[]{:S(2)}) copy-start(s32[64,128]{1,0:T(8,128)} %owner_hbm.1) | copy-start | bytes 98308
  3.9 0.8 %copy-start.3 = (s32[64,128]{1,0:T(8,128)S(1)}, s32[64,128]{1,0:T(8,128)}, u32[]{:S(2)}) copy-start(s32[64,128]{1,0:T(8,128)} %local_hbm.1) | copy-start | bytes 98308
  4.7 0.7 %copy-start.4 = (s32[64]{0:T(128)S(1)}, s32[64]{0:T(128)}, u32[]{:S(2)}) copy-start(s32[64]{0:T(128)} %lens.1) | copy-start | bytes 772

commit v2 on v1

--- a/solution.py
+++ b/solution.py
@@ -213,11 +213,11 @@
         heads = kv_local * group
         part = (group + 1) * rows
         bf16, f32 = jnp.bfloat16, jnp.float32
-        anywhere = pl.BlockSpec(memory_space=pl.ANY)
+        in_hbm = pl.BlockSpec(memory_space=pltpu.HBM)
         return pl.pallas_call(
             functools.partial(kernel, n),
             out_shape=jax.ShapeDtypeStruct((rows, heads, dim), bf16),
-            in_specs=[anywhere] * 5 + [pl.BlockSpec(memory_space=pltpu.SMEM)],
+            in_specs=[in_hbm] * 5 + [pl.BlockSpec(memory_space=pltpu.SMEM)],
             out_specs=pl.BlockSpec(memory_space=pltpu.VMEM),
             scratch_shapes=[
                 pltpu.VMEM((kv_local, pool, page_len, dim), bf16),
@@ -245,7 +245,7 @@
                 pltpu.SemaphoreType.DMA((kv_local, n)),
             ],
             compiler_params=pltpu.CompilerParams(
-                collective_id=0, has_side_effects=True, vmem_limit_bytes=48 * 1024 * 1024
+                collective_id=0, has_side_effects=True, vmem_limit_bytes=67043328
             ),
         )(queries, key_pages, value_pages, page_owner, page_local, seq_lengths)
 

time: 46.1 us -> 42.3 us (0.918)
  local copies, waits for them, and re-layouts: 5.94 us -> 1.47 us
  Pallas kernels: 39.8 us -> 40.7 us
    unnamed x11 -> x1, local copies, waits for them, and re-layouts: 5.94 us -> 1.47 us
    pallas_call x1, Pallas kernels: 39.8 us -> 40.7 us  [body(): pl.pallas_call(functools.partial(kernel, n), out_shape=jax.ShapeDtypeStru...]
where the time goes in v2:
time: 42.3 us; the launch traced here: 42.2 us
  Pallas kernels  40.7 us (96%)
  local copies, waits for them, and re-layouts  1.47 us (3%)
    pallas_call x1, Pallas kernels, body(): pl.pallas_call(functools.partial(kernel, n), out_shape=jax.ShapeDtypeStru...  40.7 us
    unnamed x1, local copies, waits for them, and re-layouts  1.47 us

profile of v2, /device:TPU:0, one launch (start us, length us, event | category | flops | bytes accessed | tf_op | source)
XLA Modules:
  0.0 42.2 jit_solution(17418987743603983085)
XLA Ops:
  0.0 40.7 %shard_map.64 = bf16[16,16,128]{2,1,0:T(8,128)(2,1)} custom-call(bf16[16,64,128]{2,1,0:T(8,128)(2,1)} %q_hbm.1, bf16[128,2,64,128]{3,2,1,0:T(8,128)(2,1)} %k_hbm.1, bf16[128,2,64,128]{3,2,1,0:T(8,128)(2,1)} %v_hbm.1, s32[64,128]{1,0:T(8,128)} %owner_hbm.1, s32[64,128]{1,0:T(8,128)} %local_hbm.1, s32[64]{0:T(128)} %lens.1), custom_call_target="tpu_custom_call" | custom-call | tf_op jit(solution)/shard_map/pallas_call | solution.py:217
  40.7 1.5 %copy.8 = bf16[16,16,128]{2,1,0:T(8,128)(2,1)} copy(bf16[16,16,128]{2,1,0:T(8,128)(2,1)} %shard_map.64) | data formatting | bytes 131072

commit v3 on v2

--- a/solution.py
+++ b/solution.py
@@ -11,7 +11,7 @@
 HQ = 64
 KVH = 8
 LANES = 128
-BLOCK = 8
+QUAD = 4
 MESH = pl.DeviceIdType.MESH
 
 score_shift = 8.0
@@ -19,7 +19,7 @@
 
 def kernel(
     n, q_hbm, k_hbm, v_hbm, owner_hbm, local_hbm, lens, out_ref,
-    kbuf, vbuf, owner, local, qg, qf, qp, fills, onehot, spread, pages, tots, stage, sbuf, rbuf, outf,
+    kbuf, vbuf, owner, local, qg, qf, qp, fills, codes, onehot, spread, pages, stage, sbuf, rbuf, outf,
     load_sem, qload_sem, kv_sem, qsend_sem, qrecv_sem, osend_sem, orecv_sem,
 ):
     me = lax.axis_index("seq")
@@ -93,9 +93,11 @@
     wide = jnp.broadcast_to(code, (pool, pool))
     tall = jnp.transpose(wide)[:seqs].astype(jnp.int32)
     wide = wide.astype(jnp.int32)
-    full = jnp.broadcast_to(wide[:, :1], (pool, LANES)) & ((1 << bits) - 1)
+    full = jnp.broadcast_to(code, (pool, LANES))
     for g in range(group):
         fills[pl.ds(g, pool, stride=group), :] = full
+    for at in range(pool * group // LANES):
+        codes[at] = jnp.transpose(fills[at * LANES : (at + 1) * LANES, :])[:8].astype(jnp.int32)
     seq_wide = wide[:, :seqs]
     onehot[...] = jnp.where(
         (seq_wide > 0) & ((seq_wide >> bits) == lax.broadcasted_iota(jnp.int32, (pool, seqs), 1)), 1.0, 0.0
@@ -104,15 +106,17 @@
         (tall > 0) & ((tall >> bits) == lax.broadcasted_iota(jnp.int32, (seqs, pool), 0)), 1.0, 0.0
     ).astype(jnp.bfloat16)
 
-    pair = 2 * group
-    span = 2 * page_len
-    row = lax.broadcasted_iota(jnp.int32, (pair, span), 0)
-    col = lax.broadcasted_iota(jnp.int32, (pair, span), 1)
-    token = jnp.where((row < group) == (col < page_len), jnp.where(col < page_len, col, col - page_len), span)
-    row_l = lax.broadcasted_iota(jnp.int32, (pair, LANES), 0)
-    col_l = lax.broadcasted_iota(jnp.int32, (pair, LANES), 1)
-    head_of = jnp.where(row_l < group, row_l, row_l - group)
-    spot = (col_l == head_of) | (col_l == head_of + group)
+    pages_in = LANES // group
+    token = lax.broadcasted_iota(jnp.int32, (page_len, LANES), 0)
+    lane_page = lax.broadcasted_iota(jnp.int32, (page_len, LANES), 1) // group
+    seq_ids = lax.broadcasted_iota(jnp.int32, (seqs, LANES), 0)
+    fold_in = lax.broadcasted_iota(jnp.int32, (LANES, LANES), 0)
+    fold_out = lax.broadcasted_iota(jnp.int32, (LANES, LANES), 1)
+    fold = jnp.where((fold_in % group == fold_out % group) & (fold_out < 2 * group), 1.0, 0.0).astype(jnp.bfloat16)
+
+    def split(value):
+        high = value.astype(jnp.bfloat16)
+        return high, (value - high.astype(jnp.float32)).astype(jnp.bfloat16)
 
     def recv(sem, kv, off, ref):
         src = lax.rem(me + n - off, n)
@@ -134,34 +138,41 @@
         for c in kv_loads[kv]:
             c.wait()
 
-        def attend(step, carry):
-            for i in range(BLOCK):
-                at = step * BLOCK + i
-                rows_at = pl.ds(pl.multiple_of(at * pair, pair), pair)
-                pages_at = pl.ds(at * 2, 2)
-                q = qp[rows_at, :].astype(jnp.bfloat16)
-                k = kbuf[kv, pages_at].reshape(span, dim)
-                v = vbuf[kv, pages_at].reshape(span, dim)
-                s = lax.dot_general(q, k, (((1,), (1,)), ((), ())), preferred_element_type=jnp.float32)
-                w = jnp.where(token < fills[rows_at, :], jnp.exp(s * scale - score_shift), 0.0)
-                total = jnp.sum(w, axis=1, keepdims=True)
-                tots[rows_at, :] = jnp.where(spot, total, 0.0)
-                pages[rows_at, :] = jnp.dot(w.astype(jnp.bfloat16), v, preferred_element_type=jnp.float32)
-            return carry
-
-        lax.fori_loop(0, pool // (2 * BLOCK), attend, 0)
+        def attend(step, sums):
+            rows_at = pl.ds(pl.multiple_of(step * LANES, LANES), LANES)
+            q = qp[rows_at, :].astype(jnp.bfloat16)
+            k = kbuf[kv, pl.ds(step * pages_in, pages_in)].reshape(pages_in * page_len, dim)
+            cross = lax.dot_general(k, q, (((1,), (1,)), ((), ())), preferred_element_type=jnp.float32)
+            s = cross[:page_len]
+            for j in range(1, pages_in):
+                s = jnp.where(lane_page == j, cross[j * page_len : (j + 1) * page_len], s)
+            code = codes[step]
+            fill = code[:1] & ((1 << bits) - 1)
+            w = jnp.where(token < fill, jnp.exp(s * scale - score_shift), 0.0)
+            total = jnp.sum(w, axis=0, keepdims=True)
+            sums += jnp.where((code[:1] >> bits) == seq_ids, total, 0.0)
+            block = jnp.concatenate([jnp.where(lane_page % QUAD == j, w, 0.0) for j in range(QUAD)], axis=0)
+            block = jnp.transpose(block).astype(jnp.bfloat16)
+            part = QUAD * group
+            for j in range(pages_in // QUAD):
+                v = vbuf[kv, pl.ds(step * pages_in + j * QUAD, QUAD)].reshape(QUAD * page_len, dim)
+                pages[pl.ds(pl.multiple_of(step * LANES + j * part, part), part), :] = jnp.dot(
+                    block[j * part : (j + 1) * part], v, preferred_element_type=jnp.float32
+                )
+            return sums
+
+        sums = lax.fori_loop(0, pool // pages_in, attend, jnp.zeros((seqs, LANES), jnp.float32))
+        high, low = split(sums)
+        tot = jnp.dot(high, fold, preferred_element_type=jnp.float32) + jnp.dot(
+            low, fold, preferred_element_type=jnp.float32
+        )
 
         def collect(value):
-            high = value.astype(jnp.bfloat16)
-            low = (value - high.astype(jnp.float32)).astype(jnp.bfloat16)
+            high, low = split(value)
             return jnp.dot(spread[...], high, preferred_element_type=jnp.float32) + jnp.dot(
                 spread[...], low, preferred_element_type=jnp.float32
             )
 
-        page_tot = tots[pl.ds(0, pool, stride=group), :]
-        for g in range(1, group):
-            page_tot += tots[pl.ds(g, pool, stride=group), :]
-        tot = collect(page_tot)
         high = tot.astype(jnp.bfloat16).astype(jnp.float32)
         lanes = lax.broadcasted_iota(jnp.int32, (seqs, LANES), 1)
         tot = jnp.where(lanes < group, high, tot - high)
@@ -227,11 +238,11 @@
                 pltpu.VMEM((kv_local, n, rows, group, dim), bf16),
                 pltpu.VMEM((seqs * group, dim), f32),
                 pltpu.VMEM((pool * group, dim), f32),
-                pltpu.VMEM((pool * group, LANES), jnp.int32),
+                pltpu.VMEM((pool * group, LANES), f32),
+                pltpu.VMEM((pool * group // LANES, 8, LANES), jnp.int32),
                 pltpu.VMEM((pool, seqs), bf16),
                 pltpu.VMEM((seqs, pool), bf16),
                 pltpu.VMEM((pool * group, dim), f32),
-                pltpu.VMEM((pool * group, LANES), f32),
                 pltpu.VMEM((kv_local, n, part, dim), f32),
                 pltpu.VMEM((kv_local, n, part, dim), bf16),
                 pltpu.VMEM((kv_local, n, part, dim), bf16),

time: 42.3 us -> 28.5 us (0.67)
  Pallas kernels: 40.7 us -> 26.8 us
    pallas_call x1, Pallas kernels: 40.7 us -> 26.8 us  [body(): pl.pallas_call(functools.partial(kernel, n), out_shape=jax.ShapeDtypeStru...]
where the time goes in v3:
time: 28.5 us; the launch traced here: 28.3 us
  Pallas kernels  26.8 us (94%)
  local copies, waits for them, and re-layouts  1.47 us (5%)
    pallas_call x1, Pallas kernels, body(): pl.pallas_call(functools.partial(kernel, n), out_shape=jax.ShapeDtypeStru...  26.8 us
    unnamed x1, local copies, waits for them, and re-layouts  1.47 us

profile of v3, /device:TPU:0, one launch (start us, length us, event | category | flops | bytes accessed | tf_op | source)
XLA Modules:
  0.0 28.3 jit_solution(14502370973015031396)
XLA Ops:
  0.0 26.8 %shard_map.64 = bf16[16,16,128]{2,1,0:T(8,128)(2,1)} custom-call(bf16[16,64,128]{2,1,0:T(8,128)(2,1)} %q_hbm.1, bf16[128,2,64,128]{3,2,1,0:T(8,128)(2,1)} %k_hbm.1, bf16[128,2,64,128]{3,2,1,0:T(8,128)(2,1)} %v_hbm.1, s32[64,128]{1,0:T(8,128)} %owner_hbm.1, s32[64,128]{1,0:T(8,128)} %local_hbm.1, s32[64]{0:T(128)} %lens.1), custom_call_target="tpu_custom_call" | custom-call | tf_op jit(solution)/shard_map/pallas_call | solution.py:228
  26.8 1.5 %copy.8 = bf16[16,16,128]{2,1,0:T(8,128)(2,1)} copy(bf16[16,16,128]{2,1,0:T(8,128)(2,1)} %shard_map.64) | data formatting | bytes 131072

commit v4 on v3

--- a/solution.py
+++ b/solution.py
@@ -161,7 +161,7 @@
                 )
             return sums
 
-        sums = lax.fori_loop(0, pool // pages_in, attend, jnp.zeros((seqs, LANES), jnp.float32))
+        sums = lax.fori_loop(0, pool // pages_in, attend, jnp.zeros((seqs, LANES), jnp.float32), unroll=2)
         high, low = split(sums)
         tot = jnp.dot(high, fold, preferred_element_type=jnp.float32) + jnp.dot(
             low, fold, preferred_element_type=jnp.float32

time: 28.5 us -> 27.8 us (0.975)
  Pallas kernels: 26.8 us -> 26.1 us
    pallas_call x1, Pallas kernels: 26.8 us -> 26.1 us  [body(): pl.pallas_call(functools.partial(kernel, n), out_shape=jax.ShapeDtypeStru...]
where the time goes in v4:
time: 27.8 us; the launch traced here: 27.6 us
  Pallas kernels  26.1 us (94%)
  local copies, waits for them, and re-layouts  1.47 us (5%)
    pallas_call x1, Pallas kernels, body(): pl.pallas_call(functools.partial(kernel, n), out_shape=jax.ShapeDtypeStru...  26.1 us
    unnamed x1, local copies, waits for them, and re-layouts  1.47 us

profile of v4, /device:TPU:0, one launch (start us, length us, event | category | flops | bytes accessed | tf_op | source)
XLA Modules:
  0.0 27.6 jit_solution(4464499608635621630)
XLA Ops:
  0.0 26.1 %shard_map.64 = bf16[16,16,128]{2,1,0:T(8,128)(2,1)} custom-call(bf16[16,64,128]{2,1,0:T(8,128)(2,1)} %q_hbm.1, bf16[128,2,64,128]{3,2,1,0:T(8,128)(2,1)} %k_hbm.1, bf16[128,2,64,128]{3,2,1,0:T(8,128)(2,1)} %v_hbm.1, s32[64,128]{1,0:T(8,128)} %owner_hbm.1, s32[64,128]{1,0:T(8,128)} %local_hbm.1, s32[64]{0:T(128)} %lens.1), custom_call_target="tpu_custom_call" | custom-call | tf_op jit(solution)/shard_map/pallas_call | solution.py:228
  26.2 1.5 %copy.8 = bf16[16,16,128]{2,1,0:T(8,128)(2,1)} copy(bf16[16,16,128]{2,1,0:T(8,128)(2,1)} %shard_map.64) | data formatting | bytes 131072
